TPU v7x, 32 devices: a whole 2x2x4 slice. The times are simulated.
32 devices in a mesh: groups: 2 (over y), sp: 4 (over z), tp: 2 (over x), dp: 2 (over core).
Axes of the slice: x: 2, y: 2, z: 4, core: 2. Of those that a mesh axis runs over, the one named last changes fastest.
Arguments:
- queries: bfloat16 [4096, 4096], P(('groups', 'tp', 'dp', 'sp')), parts along dimension 0, may hold values from -6 to 6
- keys: bfloat16 [4096, 512], P(('groups', 'tp', 'dp', 'sp')), parts along dimension 0, may hold values from -6 to 6
- values: bfloat16 [4096, 512], P(('groups', 'tp', 'dp', 'sp')), parts along dimension 0, may hold values from -6 to 6
- doc_lengths: int32 [32], P('groups'), parts along dimension 0, may hold values from 1 to 256, 2048 in all
Outputs:
- attended: bfloat16 [4096, 4096], P(('groups', 'tp', 'dp', 'sp')), parts along dimension 0
There are 2 independent parts, one for each index of `groups`. A program takes and returns all parts, laid end to end along the dimension named above; each array names one. Nothing has to cross between parts.
Inputs may be any that keep to these rules, and one draw needn't show every extreme that they name: `doc_lengths`: 16 documents whose lengths sum to 2048; the longest has exactly 256 tokens.
All inputs are finite; a program needn't handle non-finite values.
Results may differ from a plain program's by a relative error of at most 0.0038.
Values may be sent and summed in bfloat16 or wider, within the bound.
A program may use at most 64 MiB of HBM per device.

v0:
```python
import math

import jax
import jax.numpy as jnp
from jax import lax
from jax.sharding import PartitionSpec as P

HEAD_SIZE = 128


def from_behind(block, axis, distance):
    devices = range(lax.axis_size(axis))
    route = [(i - distance, i) for i in devices if i - distance in devices]
    return lax.ppermute(block, axis, route)


def local(queries, keys, values, doc_lengths):
    sp_count = lax.axis_size("sp")
    range_index = lax.axis_index("tp") * lax.axis_size("dp") + lax.axis_index("dp")
    width = queries.shape[1]
    kv_width = keys.shape[1]
    kv_heads = kv_width // HEAD_SIZE
    query_group = width // kv_width
    heads_here = width // HEAD_SIZE // sp_count
    local_width = heads_here * HEAD_SIZE
    ends = jnp.cumsum(doc_lengths)

    def doc_of(where_at):
        return jnp.sum((where_at[:, None] >= ends[None, :]).astype(jnp.int32), axis=1)

    def widen(part):
        count = part.shape[0]
        spread = jnp.broadcast_to(
            part.reshape(count, kv_heads, 1, HEAD_SIZE), (count, kv_heads, query_group, HEAD_SIZE)
        )
        return spread.reshape(count, width)

    q_heads, key_head_rows, value_head_rows = (
        lax.all_to_all(queries, "sp", split_axis=1, concat_axis=0, tiled=True),
        lax.all_to_all(widen(keys), "sp", split_axis=1, concat_axis=0, tiled=True),
        lax.all_to_all(widen(values), "sp", split_axis=1, concat_axis=0, tiled=True),
    )
    span_rows = q_heads.shape[0]
    halo_rows = span_rows // 2
    k_tail, v_tail = from_behind(
        (key_head_rows[span_rows - halo_rows :], value_head_rows[span_rows - halo_rows :]),
        ("tp", "dp"),
        1,
    )
    k_long = jnp.concatenate([k_tail, key_head_rows], axis=0).reshape(
        span_rows + halo_rows, heads_here, HEAD_SIZE
    )
    v_long = jnp.concatenate([v_tail, value_head_rows], axis=0).reshape(
        span_rows + halo_rows, heads_here, HEAD_SIZE
    )
    q_three = q_heads.reshape(span_rows, heads_here, HEAD_SIZE)
    start_offset = range_index * span_rows
    block = math.gcd(halo_rows, 512)
    q_blocks = span_rows // block
    reach = halo_rows + block
    scale = HEAD_SIZE ** (-0.5)

    def one_block(index):
        first = index * block
        q_rows = lax.dynamic_slice_in_dim(q_three, first, block, 0)
        k_rows = lax.dynamic_slice_in_dim(k_long, first, reach, 0)
        v_rows = lax.dynamic_slice_in_dim(v_long, first, reach, 0)
        q_pos = start_offset + first + jnp.arange(block, dtype=jnp.int32)
        k_pos = start_offset - halo_rows + first + jnp.arange(reach, dtype=jnp.int32)
        q_doc = doc_of(q_pos)
        k_doc = doc_of(k_pos)
        live = (
            (k_pos[None, :] <= q_pos[:, None])
            & (k_doc[None, :] == q_doc[:, None])
            & (k_pos[None, :] >= 0)
        )
        score = (
            jnp.einsum("qhd,khd->hqk", q_rows, k_rows, preferred_element_type=jnp.float32) * scale
        )
        top = jnp.max(jnp.where(live[None], score, -1e30), axis=2)
        weight = jnp.where(live[None], jnp.exp(score - top[:, :, None]), 0.0)
        total = jnp.sum(weight, axis=2)
        summed = jnp.einsum(
            "hqk,khd->qhd", weight.astype(jnp.bfloat16), v_rows, preferred_element_type=jnp.float32
        )
        return (summed / total.T[:, :, None]).astype(jnp.bfloat16).reshape(block, local_width)

    attention_output = lax.map(one_block, jnp.arange(q_blocks, dtype=jnp.int32)).reshape(
        span_rows, local_width
    )
    return lax.all_to_all(attention_output, "sp", split_axis=0, concat_axis=1, tiled=True)


def solution(mesh):
    in_specs = (
        P(("groups", "tp", "dp", "sp"), None),
        P(("groups", "tp", "dp", "sp"), None),
        P(("groups", "tp", "dp", "sp"), None),
        P("groups"),
    )
    out_specs = P(("groups", "tp", "dp", "sp"), None)
    return jax.shard_map(local, mesh=mesh, in_specs=in_specs, out_specs=out_specs, check_vma=False)
```

profile of v0, /device:TPU:1, one launch (start us, length us, event | category | flops | bytes accessed | tf_op | source)
XLA Modules:
  0.0 159.8 jit_solution(17999235760306878745)
XLA Ops:
  0.0 0.9 copy-done
  1.1 1.3 all_to_all.56
  2.4 5.4 %all-to-all-start.2 = ((bf16[128,4,1024]{2,0,1:T(8,128)(2,1)}), bf16[128,4,1024]{2,0,1:T(8,128)(2,1)S(1)}, u32[]{:S(2)}, u32[]{:S(2)}) async-start(bf16[128,4,1024]{2,0,1:T(8,128)(2,1)} %all_to_all.56), calls=%async_computation.2 | async-start | bytes 2097152 | tf_op jit(solution)/shard_map/all_to_all | solution.py:40
  7.9 25.2 %all-to-all-done.2 = bf16[128,4,1024]{2,0,1:T(8,128)(2,1)S(1)} async-done(((bf16[128,4,1024]{2,0,1:T(8,128)(2,1)}), bf16[128,4,1024]{2,0,1:T(8,128)(2,1)S(1)}, u32[]{:S(2)}, u32[]{:S(2)}) %all-to-all-start.2) | async-done | bytes 1048608 | tf_op jit(solution)/shard_map/all_to_all | solution.py:40
  33.1 1.2 broadcast_in_dim.63
  34.3 3.5 %all-to-all-start = ((bf16[128,4,1024]{0,2,1:T(8,128)(2,1)}), bf16[128,4,1024]{0,2,1:T(8,128)(2,1)S(1)}, u32[]{:S(2)}, u32[]{:S(2)}) async-start(bf16[128,4,1024]{0,2,1:T(8,128)(2,1)} %bitcast.5), calls=%async_computation | async-start | bytes 2097152 | tf_op jit(solution)/shard_map/all_to_all | solution.py:41
  37.8 1.1 copy.84
  38.9 24.2 %all-to-all-done = bf16[128,4,1024]{0,2,1:T(8,128)(2,1)S(1)} async-done(((bf16[128,4,1024]{0,2,1:T(8,128)(2,1)}), bf16[128,4,1024]{0,2,1:T(8,128)(2,1)S(1)}, u32[]{:S(2)}, u32[]{:S(2)}) %all-to-all-start) | async-done | bytes 1048608 | tf_op jit(solution)/shard_map/all_to_all | solution.py:41
  63.0 1.0 copy-done.2
  64.0 3.5 %all-to-all-start.1 = ((bf16[128,4,1024]{2,0,1:T(8,128)(2,1)}), bf16[128,4,1024]{2,0,1:T(8,128)(2,1)S(1)}, u32[]{:S(2)}, u32[]{:S(2)}) async-start(bf16[128,4,1024]{2,0,1:T(8,128)(2,1)} %bitcast.45), calls=%async_computation.1 | async-start | bytes 2097152 | tf_op jit(solution)/shard_map/all_to_all | solution.py:39
  68.4 4.4 %collective-permute-start.1 = (bf16[256,1024]{1,0:T(8,128)(2,1)}, bf16[256,1024]{1,0:T(8,128)(2,1)}, u32[]{:S(2)}, u32[]{:S(2)}) collective-permute-start(bf16[256,1024]{1,0:T(8,128)(2,1)} %bitcast.11), channel_id=1, source_target_pairs={{0,1},{1,2},{2,3},{4,5},{5,6},{6,7},{8,9},{9,10},{10,11},{12,13},{... | collective-permute-start | bytes 1572872 | tf_op jit(solution)/shard_map/ppermute | solution.py:14
  72.8 1.5 copy.52
  75.1 1.9 %collective-permute-start = (bf16[256,1024]{1,0:T(8,128)(2,1)}, bf16[256,1024]{1,0:T(8,128)(2,1)}, u32[]{:S(2)}, u32[]{:S(2)}) collective-permute-start(bf16[256,1024]{1,0:T(8,128)(2,1)} %bitcast.7), channel_id=1, source_target_pairs={{0,1},{1,2},{2,3},{4,5},{5,6},{6,7},{8,9},{9,10},{10,11},{12,13},{... | collective-permute-start | bytes 1572872 | tf_op jit(solution)/shard_map/ppermute | solution.py:14
  77.3 1.3 copy.73
  78.5 1.3 copy.75
  79.8 12.9 %all-to-all-done.1 = bf16[128,4,1024]{2,0,1:T(8,128)(2,1)S(1)} async-done(((bf16[128,4,1024]{2,0,1:T(8,128)(2,1)}), bf16[128,4,1024]{2,0,1:T(8,128)(2,1)S(1)}, u32[]{:S(2)}, u32[]{:S(2)}) %all-to-all-start.1) | async-done | bytes 1048608 | tf_op jit(solution)/shard_map/all_to_all | solution.py:39
  92.8 1.3 copy.74
  94.1 1.2 copy.56
  95.6 1.1 copy.72
  96.8 2.7 %pad_maximum_fusion = (bf16[768,8,128]{2,1,0:T(8,128)(2,1)S(1)}, bf16[768,8,128]{2,1,0:T(8,128)(2,1)}) fusion(bf16[512,8,128]{2,1,0:T(8,128)(2,1)S(1)} %bitcast.65, bf16[256,8,128]{2,1,0:T(8,128)(2,1)S(1)} %bitcast.67, bf16[512,8,128]{2,1,0:T(8,128)(2,1)} %bitcast.66, bf16[256,8,128]{2,1,0:T(8,128)(2,1)S(1)} %copy.57), kind=kLoop, calls=%fused_computation.29 | loop fusion | flops 1572864 | bytes 6291456 | tf_op jit(solution)/shard_map/concatenate | solution.py:53
  99.5 30.2 %while.12 = (s32[]{:T(128)}, bf16[2,256,1024]{2,1,0:T(8,128)(2,1)}, s32[2]{0:T(128)S(1)}, bf16[768,8,128]{2,1,0:T(8,128)(2,1)S(1)}, s32[]{:T(128)}, /*index=5*/s...) while((s32[]{:T(128)}, bf16[2,256,1024]{2,1,0:T(8,128)(2,1)}, ...), condition=%wide.region_6.7_spmd, body=%wide.region_1.6_spmd.sunk | while | flops 545297920 | bytes 27558816 | solution.py:88
  100.7 2.3 %constant_dynamic-slice_fusion.5 = (bf16[512,8,128]{2,1,0:T(8,128)(2,1)S(1)}, bf16[512,8,128]{2,1,0:T(8,128)(2,1)}) fusion(bf16[768,8,128]{2,1,0:T(8,128)(2,1)} %get-tuple-element.275, s32[]{:T(128)S(6)} %select_n.34, bf16[768,8,128]{2,1,0:T(8,128)(2,1)S(1)} %get-tuple-element.270), kind=kLoop, calls=%fused_computation.24.clone.1 | loop fusion | bytes 4194308 | tf_op jit(solution)/shard_map/while/body/eval_jaxpr/dynamic_slice | solution.py:66
  103.1 1.1 constant_dynamic-slice_fusion.6
  104.1 2.7 %fusion.39 = f32[8,256,512]{2,1,0:T(8,128)} fusion(bf16[512,8,128]{2,1,0:T(8,128)(2,1)S(1)} %get-tuple-element.235, bf16[256,8,128]{2,1,0:T(8,128)(2,1)S(1)} %constant_dynamic-slice_fusion.6), kind=kOutput, calls=%fused_computation.13.clone.1 | convolution fusion | flops 268435456 | bytes 5767168 | tf_op jit(solution)/shard_map/while/body/eval_jaxpr/qhd,khd->hqk/dot_general | solution.py:78
  107.2 5.5 %fusion.40 = (f32[8,256]{1,0:T(8,128)S(1)}, bf16[8,256,512]{2,1,0:T(8,128)(2,1)S(1)}) fusion(f32[8,256,512]{2,1,0:T(8,128)} %fusion.39, pred[256,512]{1,0:T(8,128)(4,1)S(1)} %and_and_fusion.2), kind=kOutput, calls=%fused_computation.33.clone.1 | output fusion | flops 7340543 | bytes 6430720 | tf_op jit(solution)/shard_map/while/body/eval_jaxpr/sub | solution.py:81
  113.7 0.8 constant_dynamic-update-slice_fusion.2
  115.8 2.3 %constant_dynamic-slice_fusion.5 = (bf16[512,8,128]{2,1,0:T(8,128)(2,1)S(1)}, bf16[512,8,128]{2,1,0:T(8,128)(2,1)}) fusion(bf16[768,8,128]{2,1,0:T(8,128)(2,1)} %get-tuple-element.275, s32[]{:T(128)S(6)} %select_n.34, bf16[768,8,128]{2,1,0:T(8,128)(2,1)S(1)} %get-tuple-element.270), kind=kLoop, calls=%fused_computation.24.clone.1 | loop fusion | bytes 4194308 | tf_op jit(solution)/shard_map/while/body/eval_jaxpr/dynamic_slice | solution.py:66
  118.1 1.1 constant_dynamic-slice_fusion.6
  119.2 2.7 %fusion.39 = f32[8,256,512]{2,1,0:T(8,128)} fusion(bf16[512,8,128]{2,1,0:T(8,128)(2,1)S(1)} %get-tuple-element.235, bf16[256,8,128]{2,1,0:T(8,128)(2,1)S(1)} %constant_dynamic-slice_fusion.6), kind=kOutput, calls=%fused_computation.13.clone.1 | convolution fusion | flops 268435456 | bytes 5767168 | tf_op jit(solution)/shard_map/while/body/eval_jaxpr/qhd,khd->hqk/dot_general | solution.py:78
  122.3 5.5 %fusion.40 = (f32[8,256]{1,0:T(8,128)S(1)}, bf16[8,256,512]{2,1,0:T(8,128)(2,1)S(1)}) fusion(f32[8,256,512]{2,1,0:T(8,128)} %fusion.39, pred[256,512]{1,0:T(8,128)(4,1)S(1)} %and_and_fusion.2), kind=kOutput, calls=%fused_computation.33.clone.1 | output fusion | flops 7340543 | bytes 6430720 | tf_op jit(solution)/shard_map/while/body/eval_jaxpr/sub | solution.py:81
  129.7 28.2 %all_to_all.67 = bf16[4,128,1024]{2,1,0:T(8,128)(2,1)S(1)} all-to-all(bf16[4,128,1024]{2,1,0:T(8,128)(2,1)} %bitcast.70), channel_id=1, replica_groups=mesh['groups'=2,'sp'=4,'tp'=2,'dp'=2] {'sp'}, dimensions={0} | all-to-all | bytes 2097152 | tf_op jit(solution)/shard_map/all_to_all | solution.py:91
  158.5 1.3 copy.63
  (47 shorter events, 8.0 us)
Async XLA Ops:
  0.0 0.9 copy-start
  0.0 7.8 %copy-start.5 = (bf16[128,512]{1,0:T(8,128)(2,1)S(1)}, bf16[128,512]{1,0:T(8,128)(2,1)}, u32[]{:S(2)}) copy-start(bf16[128,512]{1,0:T(8,128)(2,1)} %param.8) | copy-start | bytes 393220
  0.9 36.9 %copy-start.4 = (bf16[128,4096]{1,0:T(8,128)(2,1)S(1)}, bf16[128,4096]{1,0:T(8,128)(2,1)}, u32[]{:S(2)}) copy-start(bf16[128,4096]{1,0:T(8,128)(2,1)} %param.6) | copy-start | bytes 3145732
  2.4 30.7 %all-to-all-start.2 = ((bf16[128,4,1024]{2,0,1:T(8,128)(2,1)}), bf16[128,4,1024]{2,0,1:T(8,128)(2,1)S(1)}, u32[]{:S(2)}, u32[]{:S(2)}) async-start(bf16[128,4,1024]{2,0,1:T(8,128)(2,1)} %all_to_all.56), calls=%async_computation.2 | async-start | bytes 2097152 | tf_op jit(solution)/shard_map/all_to_all | solution.py:40
  34.3 28.8 %all-to-all-start = ((bf16[128,4,1024]{0,2,1:T(8,128)(2,1)}), bf16[128,4,1024]{0,2,1:T(8,128)(2,1)S(1)}, u32[]{:S(2)}, u32[]{:S(2)}) async-start(bf16[128,4,1024]{0,2,1:T(8,128)(2,1)} %bitcast.5), calls=%async_computation | async-start | bytes 2097152 | tf_op jit(solution)/shard_map/all_to_all | solution.py:41
  37.8 39.2 %copy-start.6 = (s32[16]{0:T(128)S(1)}, s32[16]{0:T(128)}, u32[]{:S(2)}) copy-start(s32[16]{0:T(128)} %param.9) | copy-start | bytes 196
  63.0 1.0 copy-start.2
  64.0 28.8 %all-to-all-start.1 = ((bf16[128,4,1024]{2,0,1:T(8,128)(2,1)}), bf16[128,4,1024]{2,0,1:T(8,128)(2,1)S(1)}, u32[]{:S(2)}, u32[]{:S(2)}) async-start(bf16[128,4,1024]{2,0,1:T(8,128)(2,1)} %bitcast.45), calls=%async_computation.1 | async-start | bytes 2097152 | tf_op jit(solution)/shard_map/all_to_all | solution.py:39
  68.4 25.7 %collective-permute-start.1 = (bf16[256,1024]{1,0:T(8,128)(2,1)}, bf16[256,1024]{1,0:T(8,128)(2,1)}, u32[]{:S(2)}, u32[]{:S(2)}) collective-permute-start(bf16[256,1024]{1,0:T(8,128)(2,1)} %bitcast.11), channel_id=1, source_target_pairs={{0,1},{1,2},{2,3},{4,5},{5,6},{6,7},{8,9},{9,10},{10,11},{12,13},{... | collective-permute-start | bytes 1572872 | tf_op jit(solution)/shard_map/ppermute | solution.py:14
  75.1 20.6 %collective-permute-start = (bf16[256,1024]{1,0:T(8,128)(2,1)}, bf16[256,1024]{1,0:T(8,128)(2,1)}, u32[]{:S(2)}, u32[]{:S(2)}) collective-permute-start(bf16[256,1024]{1,0:T(8,128)(2,1)} %bitcast.7), channel_id=1, source_target_pairs={{0,1},{1,2},{2,3},{4,5},{5,6},{6,7},{8,9},{9,10},{10,11},{12,13},{... | collective-permute-start | bytes 1572872 | tf_op jit(solution)/shard_map/ppermute | solution.py:14
  78.5 18.3 %copy-start.3 = (bf16[64,8,8,128]{3,2,1,0:T(8,128)(2,1)S(1)}, bf16[64,8,8,128]{3,2,1,0:T(8,128)(2,1)}, u32[]{:S(2)}) copy-start(bf16[64,8,8,128]{3,2,1,0:T(8,128)(2,1)} %copy.73) | copy-start | bytes 3145732
  107.2 5.5 %copy-start.1 = (bf16[512,8,128]{2,1,0:T(8,128)(2,1)S(1)}, bf16[512,8,128]{2,1,0:T(8,128)(2,1)}, u32[]{:S(2)}) copy-start(bf16[512,8,128]{2,1,0:T(8,128)(2,1)} %get-tuple-element.237) | copy-start | bytes 3145732 | tf_op jit(solution)/shard_map/while
  122.3 5.5 %copy-start.1 = (bf16[512,8,128]{2,1,0:T(8,128)(2,1)S(1)}, bf16[512,8,128]{2,1,0:T(8,128)(2,1)}, u32[]{:S(2)}) copy-start(bf16[512,8,128]{2,1,0:T(8,128)(2,1)} %get-tuple-element.237) | copy-start | bytes 3145732 | tf_op jit(solution)/shard_map/while
where the time goes:
time: 163 us; the launch traced here: 160 us
  waiting for transfers between devices  62.3 us (38%)
  blocking collectives  28.2 us (17%)
  local copies, waits for them, and re-layouts  27.5 us (17%)
  starting transfers between devices  18.7 us (11%)
  other arithmetic  14.6 us (9%)
  matrix products  6.94 us (4%)
    all_to_all x1, blocking collectives, local(): lax.all_to_all(attention_output, 'sp', split_axis=0, concat_axis=1, tiled...  28.2 us
    all_to_all x1, waiting for transfers between devices, local(): lax.all_to_all(widen(keys), 'sp', split_axis=1, concat_axis=0, tiled=True)  25.2 us
    all_to_all x1, waiting for transfers between devices, local(): lax.all_to_all(widen(values), 'sp', split_axis=1, concat_axis=0, tiled=True)  24.2 us
    all_to_all x1, waiting for transfers between devices, local(): lax.all_to_all(queries, 'sp', split_axis=1, concat_axis=0, tiled=True)  12.9 us
    sub x2, other arithmetic, one_block(): weight = jnp.where(live[None], jnp.exp(score - top[:, :, None]), 0.0)  11 us
    unnamed x16, local copies, waits for them, and re-layouts  6.87 us
    ppermute x2, starting transfers between devices, from_behind(): return lax.ppermute(block, axis, route)  6.3 us
    all_to_all x1, starting transfers between devices, local(): lax.all_to_all(widen(keys), 'sp', split_axis=1, concat_axis=0, tiled=True)  5.41 us
  transfers between devices with their start and end apart: 5, of which 3 were waited for; matrix products, arithmetic and copies ran while one was open for 6% of the time, Pallas kernels for 0%

commit v1 on v0

v1 whole, which is shorter than its diff:
```python
import functools
import math

import jax
import jax.numpy as jnp
from jax import lax
from jax.experimental import pallas as pl
from jax.experimental.pallas import tpu as pltpu
from jax.sharding import PartitionSpec as P

HEAD_SIZE = 128
MESH = pl.DeviceIdType.MESH
DEAD = -1e30


def place(index, dp_count, sp_count):
    return {
        "tp": index // (dp_count * sp_count),
        "dp": (index // sp_count) % dp_count,
        "sp": index % sp_count,
    }


def kernel(
    sizes, q_hbm, k_hbm, v_hbm, lengths, out_hbm,
    q_buf, held, bias, out_buf, q_sem, kv_sem, send_sem, recv_sem, out_sem,
):
    tp_count, dp_count, sp_count, hops, heads, group = sizes
    rows = q_hbm.shape[0]
    width = group * HEAD_SIZE
    blocks = tp_count * dp_count * sp_count
    me = (lax.axis_index("tp") * dp_count + lax.axis_index("dp")) * sp_count + lax.axis_index("sp")
    right = place(lax.rem(me + 1, blocks), dp_count, sp_count)
    left = place(lax.rem(me + blocks - 1, blocks), dp_count, sp_count)

    def load(source, which, head):
        columns = pl.ds(head * HEAD_SIZE, HEAD_SIZE)
        return pltpu.make_async_copy(
            source.at[:, columns], held.at[0, head, which], kv_sem.at[head, which]
        )

    def load_q(head):
        columns = pl.ds(head * width, width)
        return pltpu.make_async_copy(q_hbm.at[:, columns], q_buf.at[:, columns], q_sem.at[head])

    def store(head):
        columns = pl.ds(head * width, width)
        return pltpu.make_async_copy(out_buf.at[:, columns], out_hbm.at[:, columns], out_sem.at[head])

    def send(hop, head):
        return pltpu.make_async_remote_copy(
            src_ref=held.at[hop, head],
            dst_ref=held.at[hop + 1, head],
            send_sem=send_sem.at[hop, head],
            recv_sem=recv_sem.at[hop, head],
            device_id=right,
            device_id_type=MESH,
        )

    for head in range(heads):
        load(k_hbm, 0, head).start()
        load(v_hbm, 1, head).start()
    for head in range(heads):
        load_q(head).start()

    barrier = pltpu.get_barrier_semaphore()
    for neighbour in (left, right):
        pl.semaphore_signal(barrier, inc=1, device_id=neighbour, device_id_type=MESH)
    pl.semaphore_wait(barrier, 2)

    for head in range(heads):
        load(k_hbm, 0, head).wait()
        load(v_hbm, 1, head).wait()
        send(0, head).start()

    base = me * rows
    position = base + lax.broadcasted_iota(jnp.int32, (rows, rows), 0)
    column = lax.broadcasted_iota(jnp.int32, (rows, rows), 1)
    first = jnp.zeros((rows, rows), jnp.int32)
    end = jnp.int32(0)
    for entry in range(lengths.shape[0]):
        end = end + lengths[entry]
        first = jnp.where(position >= end, end, first)
    for hop in range(hops + 1):
        key_position = base - hop * rows + column
        live = (key_position >= first) & (key_position <= position)
        bias[:, hop * rows : (hop + 1) * rows] = jnp.where(live, 0.0, DEAD)

    for hop in range(1, hops):
        for head in range(heads):
            send(hop - 1, head).wait_recv()
            send(hop, head).start()

    factor = HEAD_SIZE ** (-0.5) * math.log2(math.e)
    span = (hops + 1) * rows
    for head in range(heads):
        send(hops - 1, head).wait_recv()
        load_q(head).wait()
        k_all = held[:, head, 0].reshape(span, HEAD_SIZE)
        v_all = held[:, head, 1].reshape(span, HEAD_SIZE)
        for member in range(group):
            place_at = head * width + member * HEAD_SIZE
            q_rows = q_buf[:, place_at : place_at + HEAD_SIZE]
            score = lax.dot_general(
                q_rows, k_all, (((1,), (1,)), ((), ())), preferred_element_type=jnp.float32
            ) + bias[...]
            top = jnp.max(score, axis=1, keepdims=True)
            weight = jnp.exp2((score - top) * factor)
            total = jnp.sum(weight, axis=1, keepdims=True)
            summed = jnp.dot(weight.astype(jnp.bfloat16), v_all, preferred_element_type=jnp.float32)
            out_buf[:, place_at : place_at + HEAD_SIZE] = (summed / total).astype(jnp.bfloat16)
        store(head).start()

    for hop in range(hops):
        for head in range(heads):
            send(hop, head).wait_send()
    for head in range(heads):
        store(head).wait()


def solution(mesh):
    tp_count, dp_count, sp_count = (mesh.shape[axis] for axis in ("tp", "dp", "sp"))
    hops = max(sp_count // 2, 1)

    def local(queries, keys, values, doc_lengths):
        rows, width = queries.shape
        heads = keys.shape[1] // HEAD_SIZE
        group = width // keys.shape[1]
        sizes = (tp_count, dp_count, sp_count, hops, heads, group)
        hbm = pl.BlockSpec(memory_space=pl.ANY)
        return pl.pallas_call(
            functools.partial(kernel, sizes),
            out_shape=jax.ShapeDtypeStruct((rows, width), jnp.bfloat16),
            in_specs=[hbm, hbm, hbm, pl.BlockSpec(memory_space=pltpu.SMEM)],
            out_specs=hbm,
            scratch_shapes=[
                pltpu.VMEM((rows, width), jnp.bfloat16),
                pltpu.VMEM((hops + 1, heads, 2, rows, HEAD_SIZE), jnp.bfloat16),
                pltpu.VMEM((rows, (hops + 1) * rows), jnp.float32),
                pltpu.VMEM((rows, width), jnp.bfloat16),
                pltpu.SemaphoreType.DMA((heads,)),
                pltpu.SemaphoreType.DMA((heads, 2)),
                pltpu.SemaphoreType.DMA((hops, heads)),
                pltpu.SemaphoreType.DMA((hops, heads)),
                pltpu.SemaphoreType.DMA((heads,)),
            ],
            compiler_params=pltpu.CompilerParams(collective_id=0, has_side_effects=True),
        )(queries, keys, values, doc_lengths)

    spec = P(("groups", "tp", "dp", "sp"), None)
    return jax.shard_map(
        local, mesh=mesh, in_specs=(spec, spec, spec, P("groups")), out_specs=spec, check_vma=False
    )
```

time: 163 us -> 27 us (0.17); the launches traced: 160 us -> 26.8 us
  waiting for transfers between devices: 62.3 us -> 0 us
  blocking collectives: 28.2 us -> 0 us
  local copies, waits for them, and re-layouts: 27.5 us -> 2.29 us
  Pallas kernels: 0 us -> 24.5 us
  starting transfers between devices: 18.7 us -> 0 us
  other arithmetic: 14.6 us -> 0 us
  matrix products: 6.94 us -> 0 us
    all_to_all x3 -> x0, waiting for transfers between devices: 62.3 us -> none  [the longest x1 25.2 us: local(): lax.all_to_all(widen(keys), 'sp', split_axis=1, concat_axis=0, tiled=True)]
    all_to_all x1 -> x0, blocking collectives: 28.2 us -> none  [local(): lax.all_to_all(attention_output, 'sp', split_axis=0, concat_axis=1, tiled...]
    pallas_call x0 -> x1, Pallas kernels: none -> 24.5 us  [local(): pl.pallas_call(functools.partial(kernel, sizes), out_shape=jax.ShapeDtype...]
    all_to_all x3 -> x0, starting transfers between devices: 12.4 us -> none  [the longest x1 5.41 us: local(): lax.all_to_all(widen(keys), 'sp', split_axis=1, concat_axis=0, tiled=True)]
    sub x2 -> x0, other arithmetic: 11 us -> none  [one_block(): weight = jnp.where(live[None], jnp.exp(score - top[:, :, None]), 0.0)]
    dynamic_slice x6 -> x0, local copies, waits for them, and re-layouts: 8 us -> none  [the longest x2 4.64 us: one_block(): k_rows = lax.dynamic_slice_in_dim(k_long, first, reach, 0)]
    dot_general x4 -> x0, matrix products: 6.94 us -> none  [the longest x2 5.31 us: one_block(): jnp.einsum('qhd,khd->hqk', q_rows, k_rows, preferred_element_type=jnp.flo...]
    ppermute x2 -> x0, starting transfers between devices: 6.3 us -> none  [from_behind(): return lax.ppermute(block, axis, route)]
  transfers between devices with their start and end apart: 5 -> 0, of which waited for: 3 -> 0; matrix products, arithmetic and copies ran while one was open for 6% -> 0% of each run, Pallas kernels for 0% -> 0%
where the time goes in v1:
time: 27 us; the launch traced here: 26.8 us
  Pallas kernels  24.5 us (91%)
  local copies, waits for them, and re-layouts  2.29 us (8%)
    pallas_call x1, Pallas kernels, local(): pl.pallas_call(functools.partial(kernel, sizes), out_shape=jax.ShapeDtype...  24.5 us
    unnamed x1, local copies, waits for them, and re-layouts  2.29 us

profile of v1, /device:TPU:1, one launch (start us, length us, event | category | flops | bytes accessed | tf_op | source)
XLA Modules:
  0.0 26.8 jit_solution(2235292034813858268)
XLA Ops:
  0.0 24.5 %shard_map.46 = bf16[128,4096]{1,0:T(8,128)(2,1)} custom-call(bf16[128,4096]{1,0:T(8,128)(2,1)} %q_hbm.1, bf16[128,512]{1,0:T(8,128)(2,1)} %k_hbm.1, bf16[128,512]{1,0:T(8,128)(2,1)} %v_hbm.1, s32[16]{0:T(128)} %lengths.1), custom_call_target="tpu_custom_call" | custom-call | tf_op jit(solution)/shard_map/pallas_call | solution.py:131
  24.5 2.3 %copy.6 = bf16[128,4096]{1,0:T(8,128)(2,1)} copy(bf16[128,4096]{1,0:T(8,128)(2,1)} %shard_map.46) | data formatting | bytes 2097152

commit v2 on v1

--- a/solution.py
+++ b/solution.py
@@ -74,17 +74,18 @@
         send(0, head).start()
 
     base = me * rows
-    position = base + lax.broadcasted_iota(jnp.int32, (rows, rows), 0)
+    row = lax.broadcasted_iota(jnp.int32, (rows, rows), 0)
     column = lax.broadcasted_iota(jnp.int32, (rows, rows), 1)
+    near = column <= row
     first = jnp.zeros((rows, rows), jnp.int32)
     end = jnp.int32(0)
     for entry in range(lengths.shape[0]):
         end = end + lengths[entry]
-        first = jnp.where(position >= end, end, first)
-    for hop in range(hops + 1):
-        key_position = base - hop * rows + column
-        live = (key_position >= first) & (key_position <= position)
-        bias[:, hop * rows : (hop + 1) * rows] = jnp.where(live, 0.0, DEAD)
+        first = jnp.where(base + row >= end, end, first)
+    mixed_position = base + column - jnp.where(near, 0, hops * rows)
+    bias[0] = jnp.where(mixed_position >= first, 0.0, DEAD)
+    for hop in range(1, hops):
+        bias[hop] = jnp.where(base - hop * rows + column >= first, 0.0, DEAD)
 
     for hop in range(1, hops):
         for head in range(heads):
@@ -93,22 +94,31 @@
 
     factor = HEAD_SIZE ** (-0.5) * math.log2(math.e)
     span = (hops + 1) * rows
+    batch = math.gcd(group, 8)
     for head in range(heads):
         send(hops - 1, head).wait_recv()
         load_q(head).wait()
         k_all = held[:, head, 0].reshape(span, HEAD_SIZE)
         v_all = held[:, head, 1].reshape(span, HEAD_SIZE)
-        for member in range(group):
-            place_at = head * width + member * HEAD_SIZE
-            q_rows = q_buf[:, place_at : place_at + HEAD_SIZE]
+        for member in range(0, group, batch):
+            at = [head * width + (member + other) * HEAD_SIZE for other in range(batch)]
+            q_rows = jnp.concatenate([q_buf[:, a : a + HEAD_SIZE] for a in at], axis=0)
             score = lax.dot_general(
                 q_rows, k_all, (((1,), (1,)), ((), ())), preferred_element_type=jnp.float32
-            ) + bias[...]
-            top = jnp.max(score, axis=1, keepdims=True)
-            weight = jnp.exp2((score - top) * factor)
-            total = jnp.sum(weight, axis=1, keepdims=True)
-            summed = jnp.dot(weight.astype(jnp.bfloat16), v_all, preferred_element_type=jnp.float32)
-            out_buf[:, place_at : place_at + HEAD_SIZE] = (summed / total).astype(jnp.bfloat16)
+            ).reshape(batch, rows, span)
+            parts = [score[:, :, hop * rows : (hop + 1) * rows] for hop in range(hops + 1)]
+            mixed = jnp.where(near, parts[0], parts[hops])
+            parts = [part + bias[hop] for hop, part in enumerate([mixed] + parts[1:hops])]
+            top = jnp.max(functools.reduce(jnp.maximum, parts), axis=2, keepdims=True)
+            weights = [jnp.exp2((part - top) * factor) for part in parts]
+            total = jnp.sum(sum(weights[1:], weights[0]), axis=2, keepdims=True)
+            ends = [jnp.where(near, weights[0], 0.0), jnp.where(near, 0.0, weights[0])]
+            weight = jnp.concatenate([ends[0]] + weights[1:] + [ends[1]], axis=2)
+            weight = weight.astype(jnp.bfloat16).reshape(batch * rows, span)
+            summed = jnp.dot(weight, v_all, preferred_element_type=jnp.float32)
+            result = (summed.reshape(batch, rows, HEAD_SIZE) / total).astype(jnp.bfloat16)
+            for other, a in enumerate(at):
+                out_buf[:, a : a + HEAD_SIZE] = result[other]
         store(head).start()
 
     for hop in range(hops):
@@ -136,7 +146,7 @@
             scratch_shapes=[
                 pltpu.VMEM((rows, width), jnp.bfloat16),
                 pltpu.VMEM((hops + 1, heads, 2, rows, HEAD_SIZE), jnp.bfloat16),
-                pltpu.VMEM((rows, (hops + 1) * rows), jnp.float32),
+                pltpu.VMEM((hops, rows, rows), jnp.float32),
                 pltpu.VMEM((rows, width), jnp.bfloat16),
                 pltpu.SemaphoreType.DMA((heads,)),
                 pltpu.SemaphoreType.DMA((heads, 2)),

time: 27 us -> 22.6 us (0.84)
  Pallas kernels: 24.5 us -> 20.1 us
    pallas_call x1, Pallas kernels: 24.5 us -> 20.1 us  [local(): pl.pallas_call(functools.partial(kernel, sizes), out_shape=jax.ShapeDtype...]
where the time goes in v2:
time: 22.6 us; the launch traced here: 22.4 us
  Pallas kernels  20.1 us (89%)
  local copies, waits for them, and re-layouts  2.29 us (10%)
    pallas_call x1, Pallas kernels, local(): pl.pallas_call(functools.partial(kernel, sizes), out_shape=jax.ShapeDtype...  20.1 us
    unnamed x1, local copies, waits for them, and re-layouts  2.29 us

profile of v2, /device:TPU:1, one launch (start us, length us, event | category | flops | bytes accessed | tf_op | source)
XLA Modules:
  0.0 22.4 jit_solution(13118558122927465719)
XLA Ops:
  0.0 20.1 %shard_map.46 = bf16[128,4096]{1,0:T(8,128)(2,1)} custom-call(bf16[128,4096]{1,0:T(8,128)(2,1)} %q_hbm.1, bf16[128,512]{1,0:T(8,128)(2,1)} %k_hbm.1, bf16[128,512]{1,0:T(8,128)(2,1)} %v_hbm.1, s32[16]{0:T(128)} %lengths.1), custom_call_target="tpu_custom_call" | custom-call | tf_op jit(solution)/shard_map/pallas_call | solution.py:141
  20.1 2.3 %copy.6 = bf16[128,4096]{1,0:T(8,128)(2,1)} copy(bf16[128,4096]{1,0:T(8,128)(2,1)} %shard_map.46) | data formatting | bytes 2097152

commit v3 on v2

--- a/solution.py
+++ b/solution.py
@@ -22,8 +22,8 @@
 
 
 def kernel(
-    sizes, q_hbm, k_hbm, v_hbm, lengths, out_hbm,
-    q_buf, held, bias, out_buf, q_sem, kv_sem, send_sem, recv_sem, out_sem,
+    sizes, q_hbm, k_hbm, v_hbm, lengths_hbm, out_buf,
+    q_buf, held, bias, lengths, q_sem, kv_sem, send_sem, recv_sem, lengths_sem,
 ):
     tp_count, dp_count, sp_count, hops, heads, group = sizes
     rows = q_hbm.shape[0]
@@ -43,10 +43,6 @@
         columns = pl.ds(head * width, width)
         return pltpu.make_async_copy(q_hbm.at[:, columns], q_buf.at[:, columns], q_sem.at[head])
 
-    def store(head):
-        columns = pl.ds(head * width, width)
-        return pltpu.make_async_copy(out_buf.at[:, columns], out_hbm.at[:, columns], out_sem.at[head])
-
     def send(hop, head):
         return pltpu.make_async_remote_copy(
             src_ref=held.at[hop, head],
@@ -57,22 +53,45 @@
             device_id_type=MESH,
         )
 
+    def start_send(hop, head):
+        @pl.when((me >= hop) & (me < blocks - 1))
+        def _():
+            send(hop, head).start()
+
+    def wait_receive(hop, head):
+        @pl.when(me >= hop)
+        def _():
+            send(hop - 1, head).wait_recv()
+
+    get_lengths = pltpu.make_async_copy(lengths_hbm, lengths, lengths_sem)
     for head in range(heads):
         load(k_hbm, 0, head).start()
         load(v_hbm, 1, head).start()
     for head in range(heads):
         load_q(head).start()
+    get_lengths.start()
 
     barrier = pltpu.get_barrier_semaphore()
-    for neighbour in (left, right):
-        pl.semaphore_signal(barrier, inc=1, device_id=neighbour, device_id_type=MESH)
-    pl.semaphore_wait(barrier, 2)
+
+    @pl.when(me > 0)
+    def _():
+        pl.semaphore_signal(barrier, inc=1, device_id=left, device_id_type=MESH)
+
+    @pl.when(me < blocks - 1)
+    def _():
+        pl.semaphore_wait(barrier, 1)
 
     for head in range(heads):
         load(k_hbm, 0, head).wait()
         load(v_hbm, 1, head).wait()
-        send(0, head).start()
+        start_send(0, head)
+    for hop in range(1, hops + 1):
 
+        @pl.when(me < hop)
+        def _():
+            held[hop] = jnp.zeros_like(held[hop])
+
+    get_lengths.wait()
     base = me * rows
     row = lax.broadcasted_iota(jnp.int32, (rows, rows), 0)
     column = lax.broadcasted_iota(jnp.int32, (rows, rows), 1)
@@ -89,14 +108,14 @@
 
     for hop in range(1, hops):
         for head in range(heads):
-            send(hop - 1, head).wait_recv()
-            send(hop, head).start()
+            wait_receive(hop, head)
+            start_send(hop, head)
 
     factor = HEAD_SIZE ** (-0.5) * math.log2(math.e)
     span = (hops + 1) * rows
     batch = math.gcd(group, 8)
     for head in range(heads):
-        send(hops - 1, head).wait_recv()
+        wait_receive(hops, head)
         load_q(head).wait()
         k_all = held[:, head, 0].reshape(span, HEAD_SIZE)
         v_all = held[:, head, 1].reshape(span, HEAD_SIZE)
@@ -119,13 +138,13 @@
             result = (summed.reshape(batch, rows, HEAD_SIZE) / total).astype(jnp.bfloat16)
             for other, a in enumerate(at):
                 out_buf[:, a : a + HEAD_SIZE] = result[other]
-        store(head).start()
 
     for hop in range(hops):
         for head in range(heads):
-            send(hop, head).wait_send()
-    for head in range(heads):
-        store(head).wait()
+
+            @pl.when((me >= hop) & (me < blocks - 1))
+            def _():
+                send(hop, head).wait_send()
 
 
 def solution(mesh):
@@ -137,24 +156,24 @@
         heads = keys.shape[1] // HEAD_SIZE
         group = width // keys.shape[1]
         sizes = (tp_count, dp_count, sp_count, hops, heads, group)
-        hbm = pl.BlockSpec(memory_space=pl.ANY)
+        hbm = pl.BlockSpec(memory_space=pltpu.HBM)
         return pl.pallas_call(
             functools.partial(kernel, sizes),
             out_shape=jax.ShapeDtypeStruct((rows, width), jnp.bfloat16),
-            in_specs=[hbm, hbm, hbm, pl.BlockSpec(memory_space=pltpu.SMEM)],
-            out_specs=hbm,
+            in_specs=[hbm, hbm, hbm, hbm],
+            out_specs=pl.BlockSpec(memory_space=pltpu.VMEM),
             scratch_shapes=[
                 pltpu.VMEM((rows, width), jnp.bfloat16),
                 pltpu.VMEM((hops + 1, heads, 2, rows, HEAD_SIZE), jnp.bfloat16),
                 pltpu.VMEM((hops, rows, rows), jnp.float32),
-                pltpu.VMEM((rows, width), jnp.bfloat16),
+                pltpu.SMEM(doc_lengths.shape, jnp.int32),
                 pltpu.SemaphoreType.DMA((heads,)),
                 pltpu.SemaphoreType.DMA((heads, 2)),
                 pltpu.SemaphoreType.DMA((hops, heads)),
                 pltpu.SemaphoreType.DMA((hops, heads)),
-                pltpu.SemaphoreType.DMA((heads,)),
+                pltpu.SemaphoreType.DMA,
             ],
-            compiler_params=pltpu.CompilerParams(collective_id=0, has_side_effects=True),
+            compiler_params=pltpu.CompilerParams(collective_id=0, has_side_effects=True, vmem_limit_bytes=32 << 20),
         )(queries, keys, values, doc_lengths)
 
     spec = P(("groups", "tp", "dp", "sp"), None)

time: 22.6 us -> 22.6 us (level)
  Pallas kernels: 20.1 us -> 17.7 us
  local copies, waits for them, and re-layouts: 2.29 us -> 4.66 us
    pallas_call x1, Pallas kernels: 20.1 us -> 17.7 us  [local(): pl.pallas_call(functools.partial(kernel, sizes), out_shape=jax.ShapeDtype...]
    unnamed x1 -> x9, local copies, waits for them, and re-layouts: 2.29 us -> 4.66 us
where the time goes in v3:
time: 22.6 us; the launch traced here: 22.4 us
  Pallas kernels  17.7 us (78%)
  local copies, waits for them, and re-layouts  4.66 us (21%)
    pallas_call x1, Pallas kernels, local(): pl.pallas_call(functools.partial(kernel, sizes), out_shape=jax.ShapeDtype...  17.7 us
    unnamed x9, local copies, waits for them, and re-layouts  4.66 us

profile of v3, /device:TPU:1, one launch (start us, length us, event | category | flops | bytes accessed | tf_op | source)
XLA Modules:
  0.0 22.4 jit_solution(15677070124408313313)
XLA Ops:
  0.0 0.0 copy-start
  0.0 1.2 %copy-done = bf16[128,4096]{1,0:T(8,128)(2,1)S(1)} copy-done((bf16[128,4096]{1,0:T(8,128)(2,1)S(1)}, bf16[128,4096]{1,0:T(8,128)(2,1)}, u32[]{:S(2)}) %copy-start) | copy-done | bytes 1048600
  1.2 0.0 copy-start.1
  1.2 0.9 %copy-done.1 = bf16[128,512]{1,0:T(8,128)(2,1)S(1)} copy-done((bf16[128,512]{1,0:T(8,128)(2,1)S(1)}, bf16[128,512]{1,0:T(8,128)(2,1)}, u32[]{:S(2)}) %copy-start.1) | copy-done | bytes 131096
  2.1 0.0 copy-start.2
  2.1 0.9 %copy-done.2 = bf16[128,512]{1,0:T(8,128)(2,1)S(1)} copy-done((bf16[128,512]{1,0:T(8,128)(2,1)S(1)}, bf16[128,512]{1,0:T(8,128)(2,1)}, u32[]{:S(2)}) %copy-start.2) | copy-done | bytes 131096
  3.0 0.0 copy-start.3
  3.0 0.7 %copy-done.3 = s32[16]{0:T(128)S(1)} copy-done((s32[16]{0:T(128)S(1)}, s32[16]{0:T(128)}, u32[]{:S(2)}) %copy-start.3) | copy-done | bytes 88
  3.7 17.7 %shard_map.46 = bf16[128,4096]{1,0:T(8,128)(2,1)S(1)} custom-call(bf16[128,4096]{1,0:T(8,128)(2,1)S(1)} %copy-done, bf16[128,512]{1,0:T(8,128)(2,1)S(1)} %copy-done.1, bf16[128,512]{1,0:T(8,128)(2,1)S(1)} %copy-done.2, s32[16]{0:T(128)S(1)} %copy-done.3), custom_call_target="tpu_custom_call" | custom-call | tf_op jit(solution)/shard_map/pallas_call | solution.py:160
  21.4 1.0 %copy.6 = bf16[128,4096]{1,0:T(8,128)(2,1)} copy(bf16[128,4096]{1,0:T(8,128)(2,1)S(1)} %shard_map.46) | data formatting | bytes 2097152
Async XLA Ops:
  0.0 1.2 %copy-start = (bf16[128,4096]{1,0:T(8,128)(2,1)S(1)}, bf16[128,4096]{1,0:T(8,128)(2,1)}, u32[]{:S(2)}) copy-start(bf16[128,4096]{1,0:T(8,128)(2,1)} %q_hbm.1) | copy-start | bytes 3145732
  1.2 0.9 %copy-start.1 = (bf16[128,512]{1,0:T(8,128)(2,1)S(1)}, bf16[128,512]{1,0:T(8,128)(2,1)}, u32[]{:S(2)}) copy-start(bf16[128,512]{1,0:T(8,128)(2,1)} %k_hbm.1) | copy-start | bytes 393220
  2.1 0.9 %copy-start.2 = (bf16[128,512]{1,0:T(8,128)(2,1)S(1)}, bf16[128,512]{1,0:T(8,128)(2,1)}, u32[]{:S(2)}) copy-start(bf16[128,512]{1,0:T(8,128)(2,1)} %v_hbm.1) | copy-start | bytes 393220
  3.0 0.7 %copy-start.3 = (s32[16]{0:T(128)S(1)}, s32[16]{0:T(128)}, u32[]{:S(2)}) copy-start(s32[16]{0:T(128)} %lengths_hbm.1) | copy-start | bytes 196

commit v4 on v3

--- a/solution.py
+++ b/solution.py
@@ -23,13 +23,14 @@
 
 def kernel(
     sizes, q_hbm, k_hbm, v_hbm, lengths_hbm, out_buf,
-    q_buf, held, bias, lengths, q_sem, kv_sem, send_sem, recv_sem, lengths_sem,
+    q_buf, held, bias, lengths, q_sem, kv_sem, send_sem, recv_sem, lengths_sem, across_sem, carried, lent_sem, carried_sem,
 ):
     tp_count, dp_count, sp_count, hops, heads, group = sizes
     rows = q_hbm.shape[0]
     width = group * HEAD_SIZE
     blocks = tp_count * dp_count * sp_count
-    me = (lax.axis_index("tp") * dp_count + lax.axis_index("dp")) * sp_count + lax.axis_index("sp")
+    tp, dp, position = (lax.axis_index(axis) for axis in ("tp", "dp", "sp"))
+    me = (tp * dp_count + dp) * sp_count + position
     right = place(lax.rem(me + 1, blocks), dp_count, sp_count)
     left = place(lax.rem(me + blocks - 1, blocks), dp_count, sp_count)
 
@@ -53,8 +54,22 @@
             device_id_type=MESH,
         )
 
+    ahead = sp_count - position
+    crosses = (ahead <= hops) & (me + ahead < blocks)
+    across = place(jnp.minimum(me + ahead, blocks - 1), dp_count, sp_count)
+    edge = (dp == dp_count - 1) & (ahead <= hops)
+    lends = edge & (tp == tp_count - 2)
+    carries = edge & (tp == tp_count - 1) & (tp_count > 1)
+    lent = heads // 2
+    carrier = {"tp": jnp.minimum(tp + 1, tp_count - 1), "dp": dp, "sp": position}
+    lender = {"tp": jnp.maximum(tp - 1, 0), "dp": dp, "sp": position}
+    goal = {"tp": tp, "dp": 0, "sp": 0}
+
+    def sends(hop):
+        return (me >= hop) & (position < sp_count - 1)
+
     def start_send(hop, head):
-        @pl.when((me >= hop) & (me < blocks - 1))
+        @pl.when(sends(hop))
         def _():
             send(hop, head).start()
 
@@ -63,6 +78,57 @@
         def _():
             send(hop - 1, head).wait_recv()
 
+    def send_across(source, sem, target, distance, head):
+        return pltpu.make_async_remote_copy(
+            src_ref=source.at[head],
+            dst_ref=held.at[distance, head],
+            send_sem=sem.at[head],
+            recv_sem=recv_sem.at[distance - 1, head],
+            device_id=target,
+            device_id_type=MESH,
+        )
+
+    def lend(head):
+        return pltpu.make_async_remote_copy(
+            src_ref=held.at[0, head],
+            dst_ref=carried.at[head],
+            send_sem=across_sem.at[head],
+            recv_sem=lent_sem.at[head],
+            device_id=carrier,
+            device_id_type=MESH,
+        )
+
+    def each_lent(action):
+        @pl.when(lends)
+        def _():
+            for head in range(lent):
+                action(lend(head))
+
+    def each_across(action):
+        for distance in range(1, hops + 1):
+
+            @pl.when(crosses & (ahead == distance))
+            def _():
+                @pl.when(jnp.logical_not(lends))
+                def _():
+                    for head in range(lent):
+                        action(send_across(held.at[0], across_sem, across, distance, head))
+
+                for head in range(lent, heads):
+                    action(send_across(held.at[0], across_sem, across, distance, head))
+
+    def each_carried(action):
+        for distance in range(1, hops + 1):
+
+            @pl.when(carries & (ahead == distance))
+            def _():
+                for head in range(lent):
+                    action(head, send_across(carried, carried_sem, goal, distance, head))
+
+    def forward(head, copy):
+        lend(head).wait_recv()
+        copy.start()
+
     get_lengths = pltpu.make_async_copy(lengths_hbm, lengths, lengths_sem)
     for head in range(heads):
         load(k_hbm, 0, head).start()
@@ -73,18 +139,42 @@
 
     barrier = pltpu.get_barrier_semaphore()
 
-    @pl.when(me > 0)
+    def greet(device):
+        pl.semaphore_signal(barrier, inc=1, device_id=device, device_id_type=MESH)
+
+    @pl.when(position > 0)
     def _():
-        pl.semaphore_signal(barrier, inc=1, device_id=left, device_id_type=MESH)
-
-    @pl.when(me < blocks - 1)
+        greet(left)
+
+    for distance in range(1, hops + 1):
+
+        @pl.when((position == 0) & (me >= distance))
+        def _():
+            greet(place(jnp.maximum(me - distance, 0), dp_count, sp_count))
+
+        @pl.when((position == 0) & (dp == 0) & (tp == tp_count - 1) & (tp_count > 1))
+        def _():
+            greet({"tp": tp, "dp": dp_count - 1, "sp": sp_count - distance})
+
+    @pl.when(carries)
     def _():
-        pl.semaphore_wait(barrier, 1)
+        greet(lender)
+
+    peers = [position < sp_count - 1, crosses, lends, carries]
+    count = sum(peer.astype(jnp.int32) for peer in peers)
+    for number in range(1, len(peers) + 1):
+
+        @pl.when(count == number)
+        def _():
+            pl.semaphore_wait(barrier, number)
 
     for head in range(heads):
         load(k_hbm, 0, head).wait()
         load(v_hbm, 1, head).wait()
         start_send(0, head)
+    each_lent(lambda copy: copy.start())
+    each_across(lambda copy: copy.start())
+    each_carried(forward)
     for hop in range(1, hops + 1):
 
         @pl.when(me < hop)
@@ -142,9 +232,12 @@
     for hop in range(hops):
         for head in range(heads):
 
-            @pl.when((me >= hop) & (me < blocks - 1))
+            @pl.when(sends(hop))
             def _():
                 send(hop, head).wait_send()
+    each_lent(lambda copy: copy.wait_send())
+    each_across(lambda copy: copy.wait_send())
+    each_carried(lambda head, copy: copy.wait_send())
 
 
 def solution(mesh):
@@ -159,7 +252,7 @@
         hbm = pl.BlockSpec(memory_space=pltpu.HBM)
         return pl.pallas_call(
             functools.partial(kernel, sizes),
-            out_shape=jax.ShapeDtypeStruct((rows, width), jnp.bfloat16),
+            out_shape=pltpu.VMEM((rows, width), jnp.bfloat16),
             in_specs=[hbm, hbm, hbm, hbm],
             out_specs=pl.BlockSpec(memory_space=pltpu.VMEM),
             scratch_shapes=[
@@ -172,9 +265,13 @@
                 pltpu.SemaphoreType.DMA((hops, heads)),
                 pltpu.SemaphoreType.DMA((hops, heads)),
                 pltpu.SemaphoreType.DMA,
+                pltpu.SemaphoreType.DMA((heads,)),
+                pltpu.VMEM((max(heads // 2, 1), 2, rows, HEAD_SIZE), jnp.bfloat16),
+                pltpu.SemaphoreType.DMA((heads,)),
+                pltpu.SemaphoreType.DMA((heads,)),
             ],
             compiler_params=pltpu.CompilerParams(collective_id=0, has_side_effects=True, vmem_limit_bytes=32 << 20),
-        )(queries, keys, values, doc_lengths)
+        )(*(pltpu.with_memory_space_constraint(a, pltpu.HBM) for a in (queries, keys, values, doc_lengths)))
 
     spec = P(("groups", "tp", "dp", "sp"), None)
     return jax.shard_map(

time: 22.6 us -> 16.9 us (0.75)
  the two profiles are of different devices: /device:TPU:1 before, /device:TPU:10 now
where the time goes in v4:
time: 16.9 us; the launch traced here: 16.8 us
  Pallas kernels  15.8 us (93%)
  local copies, waits for them, and re-layouts  0.97 us (6%)
    pallas_call x1, Pallas kernels, local(): pl.pallas_call(functools.partial(kernel, sizes), out_shape=pltpu.VMEM((ro...  15.8 us
    unnamed x1, local copies, waits for them, and re-layouts  0.97 us

profile of v4, /device:TPU:10, one launch (start us, length us, event | category | flops | bytes accessed | tf_op | source)
XLA Modules:
  0.0 16.8 jit_solution(17061008123429894174)
XLA Ops:
  0.0 15.8 %shard_map.46 = bf16[128,4096]{1,0:T(8,128)(2,1)S(1)} custom-call(bf16[128,4096]{1,0:T(8,128)(2,1)} %q_hbm.1, bf16[128,512]{1,0:T(8,128)(2,1)} %k_hbm.1, bf16[128,512]{1,0:T(8,128)(2,1)} %v_hbm.1, s32[16]{0:T(128)} %lengths_hbm.1), custom_call_target="tpu_custom_call" | custom-call | tf_op jit(solution)/shard_map/pallas_call | solution.py:253
  15.8 1.0 %copy.6 = bf16[128,4096]{1,0:T(8,128)(2,1)} copy(bf16[128,4096]{1,0:T(8,128)(2,1)S(1)} %shard_map.46) | data formatting | bytes 2097152

commit v5 on v4

--- a/solution.py
+++ b/solution.py
@@ -60,7 +60,7 @@
     edge = (dp == dp_count - 1) & (ahead <= hops)
     lends = edge & (tp == tp_count - 2)
     carries = edge & (tp == tp_count - 1) & (tp_count > 1)
-    lent = heads // 2
+    own = heads - heads // 2
     carrier = {"tp": jnp.minimum(tp + 1, tp_count - 1), "dp": dp, "sp": position}
     lender = {"tp": jnp.maximum(tp - 1, 0), "dp": dp, "sp": position}
     goal = {"tp": tp, "dp": 0, "sp": 0}
@@ -80,7 +80,7 @@
 
     def send_across(source, sem, target, distance, head):
         return pltpu.make_async_remote_copy(
-            src_ref=source.at[head],
+            src_ref=source,
             dst_ref=held.at[distance, head],
             send_sem=sem.at[head],
             recv_sem=recv_sem.at[distance - 1, head],
@@ -91,7 +91,7 @@
     def lend(head):
         return pltpu.make_async_remote_copy(
             src_ref=held.at[0, head],
-            dst_ref=carried.at[head],
+            dst_ref=carried.at[head - own],
             send_sem=across_sem.at[head],
             recv_sem=lent_sem.at[head],
             device_id=carrier,
@@ -101,7 +101,7 @@
     def each_lent(action):
         @pl.when(lends)
         def _():
-            for head in range(lent):
+            for head in range(own, heads):
                 action(lend(head))
 
     def each_across(action):
@@ -109,21 +109,21 @@
 
             @pl.when(crosses & (ahead == distance))
             def _():
+                for head in range(own):
+                    action(send_across(held.at[0, head], across_sem, across, distance, head))
+
                 @pl.when(jnp.logical_not(lends))
                 def _():
-                    for head in range(lent):
-                        action(send_across(held.at[0], across_sem, across, distance, head))
-
-                for head in range(lent, heads):
-                    action(send_across(held.at[0], across_sem, across, distance, head))
+                    for head in range(own, heads):
+                        action(send_across(held.at[0, head], across_sem, across, distance, head))
 
     def each_carried(action):
         for distance in range(1, hops + 1):
 
             @pl.when(carries & (ahead == distance))
             def _():
-                for head in range(lent):
-                    action(head, send_across(carried, carried_sem, goal, distance, head))
+                for head in range(own, heads):
+                    action(head, send_across(carried.at[head - own], carried_sem, goal, distance, head))
 
     def forward(head, copy):
         lend(head).wait_recv()

time: 16.9 us -> 16.5 us (0.976)
  the two profiles are of different devices: /device:TPU:10 before, /device:TPU:1 now
where the time goes in v5:
time: 16.5 us; the launch traced here: 16.2 us
  Pallas kernels  15.2 us (92%)
  local copies, waits for them, and re-layouts  0.97 us (6%)
    pallas_call x1, Pallas kernels, local(): pl.pallas_call(functools.partial(kernel, sizes), out_shape=pltpu.VMEM((ro...  15.2 us
    unnamed x1, local copies, waits for them, and re-layouts  0.97 us

profile of v5, /device:TPU:1, one launch (start us, length us, event | category | flops | bytes accessed | tf_op | source)
XLA Modules:
  0.0 16.2 jit_solution(4760712493803765603)
XLA Ops:
  0.0 15.2 %shard_map.46 = bf16[128,4096]{1,0:T(8,128)(2,1)S(1)} custom-call(bf16[128,4096]{1,0:T(8,128)(2,1)} %q_hbm.1, bf16[128,512]{1,0:T(8,128)(2,1)} %k_hbm.1, bf16[128,512]{1,0:T(8,128)(2,1)} %v_hbm.1, s32[16]{0:T(128)} %lengths_hbm.1), custom_call_target="tpu_custom_call" | custom-call | tf_op jit(solution)/shard_map/pallas_call | solution.py:253
  15.2 1.0 %copy.6 = bf16[128,4096]{1,0:T(8,128)(2,1)} copy(bf16[128,4096]{1,0:T(8,128)(2,1)S(1)} %shard_map.46) | data formatting | bytes 2097152

commit v6 on v5

--- a/solution.py
+++ b/solution.py
@@ -21,9 +21,54 @@
     }
 
 
+def attend(rows, hops, near, bias, keys, values, q_refs, out_refs):
+    factor = HEAD_SIZE ** (-0.5) * math.log2(math.e)
+    span = (hops + 1) * rows
+    count = len(q_refs)
+    q_rows = jnp.concatenate([ref[...] for ref in q_refs], axis=0)
+    score = lax.dot_general(
+        q_rows, keys.reshape(span, HEAD_SIZE), (((1,), (1,)), ((), ())),
+        preferred_element_type=jnp.float32,
+    ).reshape(count, rows, span)
+    parts = [score[:, :, hop * rows : (hop + 1) * rows] for hop in range(hops + 1)]
+    mixed = jnp.where(near, parts[0], parts[hops])
+    parts = [part + bias[hop] for hop, part in enumerate([mixed] + parts[1:hops])]
+    top = jnp.max(functools.reduce(jnp.maximum, parts), axis=2, keepdims=True)
+    weights = [jnp.exp2((part - top) * factor) for part in parts]
+    total = jnp.sum(sum(weights[1:], weights[0]), axis=2, keepdims=True)
+    ends = [jnp.where(near, weights[0], 0.0), jnp.where(near, 0.0, weights[0])]
+    weight = jnp.concatenate([ends[0]] + weights[1:] + [ends[1]], axis=2)
+    weight = weight.astype(jnp.bfloat16).reshape(count * rows, span)
+    summed = jnp.dot(weight, values.reshape(span, HEAD_SIZE), preferred_element_type=jnp.float32)
+    result = (summed.reshape(count, rows, HEAD_SIZE) / total).astype(jnp.bfloat16)
+    for member, ref in enumerate(out_refs):
+        ref[...] = result[member]
+
+
+def finish(hops, group, part, last_kv, last_q, bias, out_hbm, buffer, sems):
+    rows, width = part.shape[0], group * HEAD_SIZE
+    done = part.shape[1] - width
+    columns = pl.ds(0, done)
+    early = pltpu.make_async_copy(part.at[:, columns], out_hbm.at[:, columns], sems.at[0])
+    if done:
+        early.start()
+    row = lax.broadcasted_iota(jnp.int32, (rows, rows), 0)
+    near = lax.broadcasted_iota(jnp.int32, (rows, rows), 1) <= row
+    at = [pl.ds(member * HEAD_SIZE, HEAD_SIZE) for member in range(group)]
+    attend(
+        rows, hops, near, bias, last_kv[:, 0], last_kv[:, 1],
+        [last_q.at[:, a] for a in at], [buffer.at[:, a] for a in at],
+    )
+    late = pltpu.make_async_copy(buffer, out_hbm.at[:, pl.ds(done, width)], sems.at[1])
+    late.start()
+    if done:
+        early.wait()
+    late.wait()
+
+
 def kernel(
-    sizes, q_hbm, k_hbm, v_hbm, lengths_hbm, out_buf,
-    q_buf, held, bias, lengths, q_sem, kv_sem, send_sem, recv_sem, lengths_sem, across_sem, carried, lent_sem, carried_sem,
+    sizes, q_hbm, k_hbm, v_hbm, lengths_hbm, out_buf, last_kv, last_q, bias,
+    q_buf, held, lengths, q_sem, kv_sem, send_sem, recv_sem, lengths_sem, across_sem, carried, lent_sem, carried_sem,
 ):
     tp_count, dp_count, sp_count, hops, heads, group = sizes
     rows = q_hbm.shape[0]
@@ -42,7 +87,8 @@
 
     def load_q(head):
         columns = pl.ds(head * width, width)
-        return pltpu.make_async_copy(q_hbm.at[:, columns], q_buf.at[:, columns], q_sem.at[head])
+        target = last_q if head == heads - 1 else q_buf.at[:, columns]
+        return pltpu.make_async_copy(q_hbm.at[:, columns], target, q_sem.at[head])
 
     def send(hop, head):
         return pltpu.make_async_remote_copy(
@@ -201,33 +247,18 @@
             wait_receive(hop, head)
             start_send(hop, head)
 
-    factor = HEAD_SIZE ** (-0.5) * math.log2(math.e)
-    span = (hops + 1) * rows
-    batch = math.gcd(group, 8)
-    for head in range(heads):
+    for head in range(heads - 1):
         wait_receive(hops, head)
         load_q(head).wait()
-        k_all = held[:, head, 0].reshape(span, HEAD_SIZE)
-        v_all = held[:, head, 1].reshape(span, HEAD_SIZE)
-        for member in range(0, group, batch):
-            at = [head * width + (member + other) * HEAD_SIZE for other in range(batch)]
-            q_rows = jnp.concatenate([q_buf[:, a : a + HEAD_SIZE] for a in at], axis=0)
-            score = lax.dot_general(
-                q_rows, k_all, (((1,), (1,)), ((), ())), preferred_element_type=jnp.float32
-            ).reshape(batch, rows, span)
-            parts = [score[:, :, hop * rows : (hop + 1) * rows] for hop in range(hops + 1)]
-            mixed = jnp.where(near, parts[0], parts[hops])
-            parts = [part + bias[hop] for hop, part in enumerate([mixed] + parts[1:hops])]
-            top = jnp.max(functools.reduce(jnp.maximum, parts), axis=2, keepdims=True)
-            weights = [jnp.exp2((part - top) * factor) for part in parts]
-            total = jnp.sum(sum(weights[1:], weights[0]), axis=2, keepdims=True)
-            ends = [jnp.where(near, weights[0], 0.0), jnp.where(near, 0.0, weights[0])]
-            weight = jnp.concatenate([ends[0]] + weights[1:] + [ends[1]], axis=2)
-            weight = weight.astype(jnp.bfloat16).reshape(batch * rows, span)
-            summed = jnp.dot(weight, v_all, preferred_element_type=jnp.float32)
-            result = (summed.reshape(batch, rows, HEAD_SIZE) / total).astype(jnp.bfloat16)
-            for other, a in enumerate(at):
-                out_buf[:, a : a + HEAD_SIZE] = result[other]
+        at = [head * width + member * HEAD_SIZE for member in range(group)]
+        attend(
+            rows, hops, near, bias, held[:, head, 0], held[:, head, 1],
+            [q_buf.at[:, pl.ds(a, HEAD_SIZE)] for a in at],
+            [out_buf.at[:, pl.ds(a, HEAD_SIZE)] for a in at],
+        )
+    load_q(heads - 1).wait()
+    wait_receive(hops, heads - 1)
+    last_kv[...] = held[:, heads - 1]
 
     for hop in range(hops):
         for head in range(heads):
@@ -250,15 +281,20 @@
         group = width // keys.shape[1]
         sizes = (tp_count, dp_count, sp_count, hops, heads, group)
         hbm = pl.BlockSpec(memory_space=pltpu.HBM)
-        return pl.pallas_call(
+        vmem = pl.BlockSpec(memory_space=pltpu.VMEM)
+        results = pl.pallas_call(
             functools.partial(kernel, sizes),
-            out_shape=pltpu.VMEM((rows, width), jnp.bfloat16),
+            out_shape=(
+                pltpu.VMEM((rows, width), jnp.bfloat16),
+                pltpu.VMEM((hops + 1, 2, rows, HEAD_SIZE), jnp.bfloat16),
+                pltpu.VMEM((rows, group * HEAD_SIZE), jnp.bfloat16),
+                pltpu.VMEM((hops, rows, rows), jnp.float32),
+            ),
             in_specs=[hbm, hbm, hbm, hbm],
-            out_specs=pl.BlockSpec(memory_space=pltpu.VMEM),
+            out_specs=(vmem,) * 4,
             scratch_shapes=[
                 pltpu.VMEM((rows, width), jnp.bfloat16),
                 pltpu.VMEM((hops + 1, heads, 2, rows, HEAD_SIZE), jnp.bfloat16),
-                pltpu.VMEM((hops, rows, rows), jnp.float32),
                 pltpu.SMEM(doc_lengths.shape, jnp.int32),
                 pltpu.SemaphoreType.DMA((heads,)),
                 pltpu.SemaphoreType.DMA((heads, 2)),
@@ -272,6 +308,17 @@
             ],
             compiler_params=pltpu.CompilerParams(collective_id=0, has_side_effects=True, vmem_limit_bytes=32 << 20),
         )(*(pltpu.with_memory_space_constraint(a, pltpu.HBM) for a in (queries, keys, values, doc_lengths)))
+        return pl.pallas_call(
+            functools.partial(finish, hops, group),
+            out_shape=jax.ShapeDtypeStruct((rows, width), jnp.bfloat16),
+            in_specs=[vmem] * 4,
+            out_specs=hbm,
+            scratch_shapes=[
+                pltpu.VMEM((rows, group * HEAD_SIZE), jnp.bfloat16),
+                pltpu.SemaphoreType.DMA((2,)),
+            ],
+            compiler_params=pltpu.CompilerParams(vmem_limit_bytes=32 << 20),
+        )(*(pltpu.with_memory_space_constraint(a, pltpu.VMEM) for a in results))
 
     spec = P(("groups", "tp", "dp", "sp"), None)
     return jax.shard_map(

time: 16.5 us -> 16.2 us (0.982)
  local copies, waits for them, and re-layouts: 0.97 us -> 0 us
  Pallas kernels: 15.2 us -> 16 us
    unnamed x1 -> x0, local copies, waits for them, and re-layouts: 0.97 us -> none
    pallas_call x1 -> x2, Pallas kernels: 15.2 us -> 16 us  [the longest x1 14.6 us: local(): pl.pallas_call(functools.partial(kernel, sizes), out_shape=(pltpu.VMEM((r...]
where the time goes in v6:
time: 16.2 us; the launch traced here: 16 us
  Pallas kernels  16 us (99%)
    pallas_call x1, Pallas kernels, local(): pl.pallas_call(functools.partial(kernel, sizes), out_shape=(pltpu.VMEM((r...  14.6 us
    pallas_call x1, Pallas kernels, local(): pl.pallas_call(functools.partial(finish, hops, group), out_shape=jax.Shap...  1.38 us

profile of v6, /device:TPU:1, one launch (start us, length us, event | category | flops | bytes accessed | tf_op | source)
XLA Modules:
  0.0 16.0 jit_solution(8533346788030532921)
XLA Ops:
  0.0 14.6 %shard_map.46 = (bf16[128,4096]{1,0:T(8,128)(2,1)S(1)}, bf16[3,2,128,128]{3,2,1,0:T(8,128)(2,1)S(1)}, bf16[128,1024]{1,0:T(8,128)(2,1)S(1)}, f32[2,128,128]{2,1,0:T(8,128)S(1)}) custom-call(bf16[128,4096]{1,0:T(8,128)(2,1)} %q_hbm.1, bf16[128,512]{1,0:T(8,128)(2,1)} %k_hbm.1, bf16[128,512]{1,0:T(8,128)(2,1)} %v_hbm.1, s32[16]{0:T(128)} %lengths_hbm.1), custom_call_target="tpu_custom_call" | custom-call | tf_op jit(solution)/shard_map/pallas_call | solution.py:285
  14.6 1.4 %shard_map.47 = bf16[128,4096]{1,0:T(8,128)(2,1)} custom-call(bf16[128,4096]{1,0:T(8,128)(2,1)S(1)} %get-tuple-element.9.part, bf16[3,2,128,128]{3,2,1,0:T(8,128)(2,1)S(1)} %get-tuple-element.10.last_kv, bf16[128,1024]{1,0:T(8,128)(2,1)S(1)} %get-tuple-element.11.last_q, f32[2,128,128]{2,1,0:T(8,128)S(1)} %get-tuple-element.12.bias), custom_call_target="tpu_custom_call" | custom-call | tf_op jit(solution)/shard_map/pallas_call | solution.py:311

commit v7 on v6

--- a/solution.py
+++ b/solution.py
@@ -176,35 +176,35 @@
         copy.start()
 
     get_lengths = pltpu.make_async_copy(lengths_hbm, lengths, lengths_sem)
+    barrier = pltpu.get_barrier_semaphore()
+
+    def greet(device):
+        pl.semaphore_signal(barrier, inc=1, device_id=device, device_id_type=MESH)
+
+    @pl.when(position > 0)
+    def _():
+        greet(left)
+
+    for distance in range(1, hops + 1):
+
+        @pl.when((position == 0) & (me >= distance))
+        def _():
+            greet(place(jnp.maximum(me - distance, 0), dp_count, sp_count))
+
+        @pl.when((position == 0) & (dp == 0) & (tp == tp_count - 1) & (tp_count > 1))
+        def _():
+            greet({"tp": tp, "dp": dp_count - 1, "sp": sp_count - distance})
+
+    @pl.when(carries)
+    def _():
+        greet(lender)
+
     for head in range(heads):
         load(k_hbm, 0, head).start()
         load(v_hbm, 1, head).start()
     for head in range(heads):
         load_q(head).start()
     get_lengths.start()
-
-    barrier = pltpu.get_barrier_semaphore()
-
-    def greet(device):
-        pl.semaphore_signal(barrier, inc=1, device_id=device, device_id_type=MESH)
-
-    @pl.when(position > 0)
-    def _():
-        greet(left)
-
-    for distance in range(1, hops + 1):
-
-        @pl.when((position == 0) & (me >= distance))
-        def _():
-            greet(place(jnp.maximum(me - distance, 0), dp_count, sp_count))
-
-        @pl.when((position == 0) & (dp == 0) & (tp == tp_count - 1) & (tp_count > 1))
-        def _():
-            greet({"tp": tp, "dp": dp_count - 1, "sp": sp_count - distance})
-
-    @pl.when(carries)
-    def _():
-        greet(lender)
 
     peers = [position < sp_count - 1, crosses, lends, carries]
     count = sum(peer.astype(jnp.int32) for peer in peers)
@@ -257,8 +257,9 @@
             [out_buf.at[:, pl.ds(a, HEAD_SIZE)] for a in at],
         )
     load_q(heads - 1).wait()
+    last_kv[:hops] = held[:hops, heads - 1]
     wait_receive(hops, heads - 1)
-    last_kv[...] = held[:, heads - 1]
+    last_kv[hops] = held[hops, heads - 1]
 
     for hop in range(hops):
         for head in range(heads):

time: 16.2 us -> 16.2 us (level)
  the two profiles are of different devices: /device:TPU:1 before, /device:TPU:3 now
where the time goes in v7:
time: 16.2 us; the launch traced here: 16.1 us
  Pallas kernels  16.1 us (99%)
    pallas_call x1, Pallas kernels, local(): pl.pallas_call(functools.partial(kernel, sizes), out_shape=(pltpu.VMEM((r...  14.7 us
    pallas_call x1, Pallas kernels, local(): pl.pallas_call(functools.partial(finish, hops, group), out_shape=jax.Shap...  1.38 us

profile of v7, /device:TPU:3, one launch (start us, length us, event | category | flops | bytes accessed | tf_op | source)
XLA Modules:
  0.0 16.1 jit_solution(4696873708470986699)
XLA Ops:
  0.0 14.7 %shard_map.46 = (bf16[128,4096]{1,0:T(8,128)(2,1)S(1)}, bf16[3,2,128,128]{3,2,1,0:T(8,128)(2,1)S(1)}, bf16[128,1024]{1,0:T(8,128)(2,1)S(1)}, f32[2,128,128]{2,1,0:T(8,128)S(1)}) custom-call(bf16[128,4096]{1,0:T(8,128)(2,1)} %q_hbm.1, bf16[128,512]{1,0:T(8,128)(2,1)} %k_hbm.1, bf16[128,512]{1,0:T(8,128)(2,1)} %v_hbm.1, s32[16]{0:T(128)} %lengths_hbm.1), custom_call_target="tpu_custom_call" | custom-call | tf_op jit(solution)/shard_map/pallas_call | solution.py:286
  14.7 1.4 %shard_map.47 = bf16[128,4096]{1,0:T(8,128)(2,1)} custom-call(bf16[128,4096]{1,0:T(8,128)(2,1)S(1)} %get-tuple-element.9.part, bf16[3,2,128,128]{3,2,1,0:T(8,128)(2,1)S(1)} %get-tuple-element.10.last_kv, bf16[128,1024]{1,0:T(8,128)(2,1)S(1)} %get-tuple-element.11.last_q, f32[2,128,128]{2,1,0:T(8,128)S(1)} %get-tuple-element.12.bias), custom_call_target="tpu_custom_call" | custom-call | tf_op jit(solution)/shard_map/pallas_call | solution.py:312
